TPU v7x, 32 devices: a whole 2x2x4 slice. The times are simulated.
32 devices in a mesh: tm: 8 (over z, core), member: 4 (over y, x).
Axes of the slice: x: 2, y: 2, z: 4, core: 2. Of those that a mesh axis runs over, the one named last changes fastest.
Arguments:
- fields: float32 [48, 48, 8192], P('member', 'tm'), may hold values from 200 to 350, as said below
Outputs:
- covariance: float32 [48, 48, 8192], P('member', None, 'tm')
Inputs may be any that keep to these rules, and one draw needn't show every extreme that they name: `fields`: month t is calendar month t mod 12.
All inputs are finite; a program needn't handle non-finite values.
Results may differ from a plain program's by a relative error of at most 0.0003.
Values sent between devices are 32-bit elements; how exact they have to be, the bound alone decides.
A program may use at most 192 MiB of HBM per device.

v0:
```python
import jax
import jax.numpy as jnp
from jax import lax
from jax.sharding import PartitionSpec as P


def monthly_anomaly(series):
    members_here, months_here, pixel_count = series.shape
    by_year = series.reshape(members_here, months_here // 12, 12, pixel_count)
    climatology = jnp.mean(by_year, axis=1, keepdims=True)
    return (by_year - climatology).reshape(members_here, months_here, pixel_count)


def cross_block(first_rows, second_rows, divisor):
    products = jnp.einsum(
        "itp,jtp->ijp",
        first_rows,
        second_rows,
        precision=lax.Precision.HIGHEST,
        preferred_element_type=jnp.float32,
    )
    return products / divisor


def per_device(fields):
    members_here, mon_here, pixel_count = fields.shape
    tm_count = lax.axis_size("tm")
    divisor = float(mon_here * tm_count - 12)
    regrouped = lax.all_to_all(
        lax.all_to_all(fields, "tm", split_axis=2, concat_axis=1, tiled=True),
        "member",
        split_axis=2,
        concat_axis=0,
        tiled=True,
    )
    anomaly = monthly_anomaly(regrouped)
    whole_block = cross_block(anomaly, anomaly, divisor)
    return lax.all_to_all(whole_block, "member", split_axis=0, concat_axis=2, tiled=True)


def solution(mesh):
    in_specs = (P("member", "tm", None),)
    out_specs = P("member", None, "tm")
    return jax.shard_map(
        per_device, mesh=mesh, in_specs=in_specs, out_specs=out_specs, check_vma=False
    )
```

profile of v0, /device:TPU:0, one launch (start us, length us, event | category | flops | bytes accessed | tf_op | source)
XLA Modules:
  0.0 288.6 jit_solution(1620361578068104155)
XLA Ops:
  0.0 17.2 %copy.42 = f32[12,6,8192]{0,1,2:T(8,128)} copy(f32[12,6,8192]{2,1,0:T(8,128)} %param.1) | data formatting | bytes 4718592 | tf_op args[0]
  17.2 18.9 %reshape.15 = f32[8,1,73728]{2,1,0:T(1,128)S(1)} reshape(f32[8192,6,12]{2,1,0:T(8,128)} %bitcast.24) | data formatting | bytes 4718592
  36.2 60.9 %all_to_all.51 = f32[8,1,73728]{2,1,0:T(1,128)} all-to-all(f32[8,1,73728]{2,1,0:T(1,128)S(1)} %reshape.15), channel_id=1, replica_groups=mesh['tm'=8,'member'=4] {'tm'}, dimensions={0} | all-to-all | bytes 4718592 | tf_op jit(solution)/shard_map/all_to_all | solution.py:30
  97.1 0.6 broadcast.10
  97.6 7.9 %reduce.1 = f32[8,73728]{1,0:T(8,128)S(1)} reduce(f32[8,1,73728]{2,1,0:T(1,128)} %all_to_all.51, f32[]{:T(128)} %broadcast.10), dimensions={1}, to_apply=%all_to_all.37.reduce_sub_computation | reduce | bytes 4718596 | tf_op jit(solution)/shard_map/all_to_all | solution.py:30
  105.6 26.8 %reshape.16 = f32[8192,6,12]{2,1,0:T(8,128)} reshape(f32[8,73728]{1,0:T(8,128)S(1)} %reduce.1) | data formatting | bytes 4718592
  132.4 19.7 %copy.43 = f32[12,6,8,1024]{3,1,2,0:T(8,128)S(1)} copy(f32[12,6,8,1024]{0,1,3,2:T(8,128)} %bitcast.23) | data formatting | bytes 4718592 | tf_op jit(solution)/shard_map/all_to_all | solution.py:30
  152.1 1.6 all_to_all.40
  153.7 7.6 %copy.44 = f32[12,48,1024]{1,0,2:T(8,128)} copy(f32[12,48,1024]{2,1,0:T(8,128)} %all_to_all.40) | data formatting | bytes 4718592 | tf_op jit(solution)/shard_map/all_to_all | solution.py:30
  161.2 8.8 %reshape.17 = f32[4,1,147456]{2,1,0:T(1,128)} reshape(f32[1024,12,48]{2,1,0:T(8,128)} %bitcast.25) | data formatting | bytes 4718592
  170.0 31.9 %all_to_all.52 = f32[4,1,147456]{2,1,0:T(1,128)S(1)} all-to-all(f32[4,1,147456]{2,1,0:T(1,128)} %reshape.17), channel_id=1, replica_groups=mesh['tm'=8,'member'=4] {'member'}, dimensions={0} | all-to-all | bytes 4718592 | tf_op jit(solution)/shard_map/all_to_all | solution.py:29
  201.9 8.3 %reduce.2 = f32[4,147456]{1,0:T(4,128)} reduce(f32[4,1,147456]{2,1,0:T(1,128)S(1)} %all_to_all.52, f32[]{:T(128)} %broadcast.10), dimensions={1}, to_apply=%all_to_all.41.reduce_sub_computation | reduce | bytes 4718596 | tf_op jit(solution)/shard_map/all_to_all | solution.py:29
  210.2 10.3 %reshape.18 = f32[1024,12,48]{2,1,0:T(8,128)} reshape(f32[4,147456]{1,0:T(4,128)} %reduce.2) | data formatting | bytes 4718592
  220.5 5.7 %copy.54 = f32[12,48,4,256]{3,2,1,0:T(4,128)S(1)} copy(f32[12,48,4,256]{1,0,3,2:T(8,128)} %bitcast.26) | data formatting | bytes 4718592 | tf_op jit(solution)/shard_map/all_to_all | solution.py:29
  226.2 0.8 reduce
  226.9 0.1 copy.55
  227.1 0.4 copy_multiply_fusion
  227.5 0.5 copy.46
  227.9 0.3 sub.11
  228.2 1.4 bitcast_subtract_fusion
  229.6 5.4 %copy.50 = f32[48,48,256]{1,0,2:T(8,128)} copy(f32[48,48,256]{2,1,0:T(8,128)S(1)} %bitcast_subtract_fusion) | data formatting | bytes 4718592 | tf_op jit(solution)/shard_map/sub | solution.py:11
  235.1 16.4 %multiply_bitcast_fusion = f32[48,48,256]{0,1,2:T(8,128)} fusion(f32[48,48,256]{1,0,2:T(8,128)} %copy.50), kind=kOutput, calls=%fused_computation | convolution fusion | flops 340328448 | bytes 4718592 | tf_op jit(solution)/shard_map/itp,jtp->ijp/dot_general | solution.py:15
  251.5 5.9 %copy.52 = f32[48,48,256]{2,1,0:T(8,128)S(1)} copy(f32[48,48,256]{0,1,2:T(8,128)} %multiply_bitcast_fusion) | data formatting | bytes 4718592 | tf_op jit(solution)/shard_map/div | solution.py:22
  257.3 29.3 %all_to_all.53 = f32[48,48,256]{2,1,0:T(8,128)S(1)} all-to-all(f32[48,48,256]{2,1,0:T(8,128)S(1)} %copy.52), channel_id=1, replica_groups=mesh['tm'=8,'member'=4] {'member'}, dimensions={0} | all-to-all | bytes 4718592 | tf_op jit(solution)/shard_map/all_to_all | solution.py:38
  286.6 1.7 copy.56
where the time goes:
time: 293 us; the launch traced here: 289 us
  local copies, waits for them, and re-layouts  131 us (45%)
  blocking collectives  122 us (42%)
  other arithmetic  18.8 us (6%)
  matrix products  16.4 us (6%)
    unnamed x6, local copies, waits for them, and re-layouts  82.1 us
    all_to_all x1, blocking collectives, per_device(): lax.all_to_all(fields, 'tm', split_axis=2, concat_axis=1, tiled=True)  60.9 us
    all_to_all x1, blocking collectives, per_device(): lax.all_to_all(lax.all_to_all(fields, 'tm', split_axis=2, concat_axis=1,...  31.9 us
    all_to_all x4, local copies, waits for them, and re-layouts, per_device(): lax.all_to_all(fields, 'tm', split_axis=2, concat_axis=1, tiled=True)  29.4 us
    all_to_all x1, blocking collectives, per_device(): lax.all_to_all(whole_block, 'member', split_axis=0, concat_axis=2, tiled=...  29.3 us
    dot_general x1, matrix products, cross_block(): jnp.einsum('itp,jtp->ijp', first_rows, second_rows, precision=lax.Precisi...  16.4 us
    all_to_all x1, other arithmetic, per_device(): lax.all_to_all(lax.all_to_all(fields, 'tm', split_axis=2, concat_axis=1,...  8.3 us
    all_to_all x1, other arithmetic, per_device(): lax.all_to_all(fields, 'tm', split_axis=2, concat_axis=1, tiled=True)  7.95 us

commit v1 on v0

--- a/solution.py
+++ b/solution.py
@@ -23,6 +23,12 @@
 
 
 def per_device(fields):
+
+    def assign_the_numbers(mat):
+        block_last = jnp.stack(jnp.split(mat, lax.axis_size("member"), axis=0))
+        reached = lax.all_to_all(block_last, "member", 0, 0)
+        return jnp.concatenate(reached, axis=2)
+
     members_here, mon_here, pixel_count = fields.shape
     tm_count = lax.axis_size("tm")
     divisor = float(mon_here * tm_count - 12)
@@ -35,7 +41,7 @@
     )
     anomaly = monthly_anomaly(regrouped)
     whole_block = cross_block(anomaly, anomaly, divisor)
-    return lax.all_to_all(whole_block, "member", split_axis=0, concat_axis=2, tiled=True)
+    return assign_the_numbers(whole_block)
 
 
 def solution(mesh):

time: 293 us -> 299 us (1.020)
  local copies, waits for them, and re-layouts: 131 us -> 137 us
    another operation x0 -> x5, local copies, waits for them, and re-layouts: none -> 12.2 us  [assign_the_numbers(): block_last = jnp.stack(jnp.split(mat, lax.axis_size('member'), axis=0))]
    div x1 -> x0, local copies, waits for them, and re-layouts: 5.86 us -> none  [cross_block(): return products / divisor]
where the time goes in v1:
time: 299 us; the launch traced here: 295 us
  local copies, waits for them, and re-layouts  137 us (46%)
  blocking collectives  122 us (41%)
  other arithmetic  20.2 us (7%)
  matrix products  15.3 us (5%)
    unnamed x6, local copies, waits for them, and re-layouts  82.2 us
    all_to_all x1, blocking collectives, per_device(): lax.all_to_all(fields, 'tm', split_axis=2, concat_axis=1, tiled=True)  60.9 us
    all_to_all x1, blocking collectives, per_device(): lax.all_to_all(lax.all_to_all(fields, 'tm', split_axis=2, concat_axis=1,...  32.1 us
    all_to_all x4, local copies, waits for them, and re-layouts, per_device(): lax.all_to_all(fields, 'tm', split_axis=2, concat_axis=1, tiled=True)  29.4 us
    all_to_all x1, blocking collectives, assign_the_numbers(): reached = lax.all_to_all(block_last, 'member', 0, 0)  29.3 us
    dot_general x1, matrix products, cross_block(): jnp.einsum('itp,jtp->ijp', first_rows, second_rows, precision=lax.Precisi...  15.3 us
    another operation x5, local copies, waits for them, and re-layouts, assign_the_numbers(): block_last = jnp.stack(jnp.split(mat, lax.axis_size('member'), axis=0))  12.2 us
    all_to_all x1, other arithmetic, per_device(): lax.all_to_all(lax.all_to_all(fields, 'tm', split_axis=2, concat_axis=1,...  8.3 us

profile of v1, /device:TPU:0, one launch (start us, length us, event | category | flops | bytes accessed | tf_op | source)
XLA Modules:
  0.0 295.2 jit_solution(9769551122418458646)
XLA Ops:
  0.0 17.2 %copy.54 = f32[12,6,8192]{0,1,2:T(8,128)} copy(f32[12,6,8192]{2,1,0:T(8,128)} %param.1) | data formatting | bytes 4718592 | tf_op args[0]
  17.2 18.9 %reshape.23 = f32[8,1,73728]{2,1,0:T(1,128)S(1)} reshape(f32[8192,6,12]{2,1,0:T(8,128)} %bitcast.30) | data formatting | bytes 4718592
  36.2 60.9 %all_to_all.38 = f32[8,1,73728]{2,1,0:T(1,128)} all-to-all(f32[8,1,73728]{2,1,0:T(1,128)S(1)} %reshape.23), channel_id=1, replica_groups=mesh['tm'=8,'member'=4] {'tm'}, dimensions={0} | all-to-all | bytes 4718592 | tf_op jit(solution)/shard_map/all_to_all | solution.py:36
  97.1 0.6 broadcast.10
  97.6 7.9 %reduce.1 = f32[8,73728]{1,0:T(8,128)S(1)} reduce(f32[8,1,73728]{2,1,0:T(1,128)} %all_to_all.38, f32[]{:T(128)} %broadcast.10), dimensions={1}, to_apply=%all_to_all.27.reduce_sub_computation | reduce | bytes 4718596 | tf_op jit(solution)/shard_map/all_to_all | solution.py:36
  105.6 26.9 %reshape.24 = f32[8192,6,12]{2,1,0:T(8,128)} reshape(f32[8,73728]{1,0:T(8,128)S(1)} %reduce.1) | data formatting | bytes 4718592
  132.4 19.7 %copy.55 = f32[12,6,8,1024]{3,1,2,0:T(8,128)S(1)} copy(f32[12,6,8,1024]{0,1,3,2:T(8,128)} %bitcast.29) | data formatting | bytes 4718592 | tf_op jit(solution)/shard_map/all_to_all | solution.py:36
  152.1 1.6 all_to_all.30
  153.7 7.6 %copy.56 = f32[12,48,1024]{1,0,2:T(8,128)} copy(f32[12,48,1024]{2,1,0:T(8,128)} %all_to_all.30) | data formatting | bytes 4718592 | tf_op jit(solution)/shard_map/all_to_all | solution.py:36
  161.3 8.8 %reshape.25 = f32[4,1,147456]{2,1,0:T(1,128)} reshape(f32[1024,12,48]{2,1,0:T(8,128)} %bitcast.31) | data formatting | bytes 4718592
  170.1 32.1 %all_to_all.39 = f32[4,1,147456]{2,1,0:T(1,128)S(1)} all-to-all(f32[4,1,147456]{2,1,0:T(1,128)} %reshape.25), channel_id=1, replica_groups=mesh['tm'=8,'member'=4] {'member'}, dimensions={0} | all-to-all | bytes 4718592 | tf_op jit(solution)/shard_map/all_to_all | solution.py:35
  202.1 8.3 %reduce.2 = f32[4,147456]{1,0:T(4,128)} reduce(f32[4,1,147456]{2,1,0:T(1,128)S(1)} %all_to_all.39, f32[]{:T(128)} %broadcast.10), dimensions={1}, to_apply=%all_to_all.31.reduce_sub_computation | reduce | bytes 4718596 | tf_op jit(solution)/shard_map/all_to_all | solution.py:35
  210.4 10.3 %reshape.26 = f32[1024,12,48]{2,1,0:T(8,128)} reshape(f32[4,147456]{1,0:T(4,128)} %reduce.2) | data formatting | bytes 4718592
  220.7 5.7 %copy.69 = f32[12,48,4,256]{3,2,1,0:T(4,128)S(1)} copy(f32[12,48,4,256]{1,0,3,2:T(8,128)} %bitcast.32) | data formatting | bytes 4718592 | tf_op jit(solution)/shard_map/all_to_all | solution.py:35
  226.4 0.8 reduce
  227.2 0.1 copy.70
  227.3 0.4 copy_multiply_fusion
  227.7 0.5 copy.58
  228.2 0.3 sub.11
  228.4 1.4 bitcast_subtract_fusion
  229.9 5.4 %copy.62 = f32[48,48,256]{1,0,2:T(8,128)} copy(f32[48,48,256]{2,1,0:T(8,128)S(1)} %bitcast_subtract_fusion) | data formatting | bytes 4718592 | tf_op jit(solution)/shard_map/sub | solution.py:11
  235.2 15.3 %multiply_bitcast_fusion = f32[48,48,256]{1,0,2:T(8,128)S(1)} fusion(f32[48,48,256]{1,0,2:T(8,128)} %copy.62), kind=kOutput, calls=%fused_computation | convolution fusion | flops 340328448 | bytes 4718592 | tf_op jit(solution)/shard_map/itp,jtp->ijp/dot_general | solution.py:15
  250.5 2.9 slice_bitcast_fusion.3
  253.4 2.3 copy.64
  255.7 2.3 copy.67
  258.0 3.1 %copy.66 = f32[1,12,48,256]{3,2,1,0:T(8,128)} copy(f32[1,12,48,256]{2,1,3,0:T(8,128)} %get-tuple-element.7) | data formatting | bytes 1179648 | tf_op jit(solution)/shard_map/stack | solution.py:28
  261.1 1.6 copy.65
  262.7 1.4 pad_maximum_fusion
  264.1 29.3 %all_to_all.40 = f32[4,12,48,256]{3,2,1,0:T(8,128)S(1)} all-to-all(f32[4,12,48,256]{3,2,1,0:T(8,128)S(1)} %pad_maximum_fusion), channel_id=1, replica_groups=mesh['tm'=8,'member'=4] {'member'}, dimensions={0} | all-to-all | bytes 4718592 | tf_op jit(solution)/shard_map/all_to_all | solution.py:29
  293.4 1.7 copy.71
